TPU v7x, 32 devices: a whole 2x2x4 slice. The times are simulated.
32 devices in a mesh: dp: 4 (over z), sp: 8 (over y, x, core).
Axes of the slice: x: 2, y: 2, z: 4, core: 2. Of those that a mesh axis runs over, the one named last changes fastest.
Arguments:
- queries_in: bfloat16 [8, 8192, 16, 128], P('dp', 'sp'), may hold values from -6 to 6
- keys_in: bfloat16 [8, 8192, 16, 128], P('dp', 'sp'), may hold values from -6 to 6
- values_in: bfloat16 [8, 8192, 16, 128], P('dp', 'sp'), may hold values from -6 to 6
- out_weight: bfloat16 [2048, 2048], P('dp'), may hold values from -0.125 to 0.125
Outputs:
- block_out: bfloat16 [8, 8192, 2048], P('dp', 'sp')
All inputs are finite; a program needn't handle non-finite values.
Results may differ from a plain program's by a relative error of at most 0.006.
Values may be sent and summed in bfloat16 or wider, within the bound.
A program may use at most 320 MiB of HBM per device.

v0:
```python
import jax
import jax.numpy as jnp
from jax import lax
from jax.sharding import PartitionSpec as P


def feature_map(values):
    wide = values.astype(jnp.float32)
    return (wide * wide + 0.1).astype(jnp.bfloat16)


def finish_heads(read, count):
    result = read * count**0.5
    return result.astype(jnp.bfloat16)


def look_up(features, state, mass):
    top = jnp.einsum(
        "bthd,bhde->bthe", features, state.astype(jnp.bfloat16), preferred_element_type=jnp.float32
    )
    bottom = jnp.einsum(
        "bthd,bhd->bth", features.astype(jnp.float32), mass, precision=lax.Precision.HIGHEST
    )
    return top / (bottom + 0.001)[..., None]


def on_device(queries_in, keys_in, values_in, out_weight):
    query_feature, key_feature = (feature_map(queries_in), feature_map(keys_in))
    count = queries_in.shape[1] * lax.axis_size("sp")
    part_state = jnp.einsum(
        "bthd,bthe->bhde", key_feature, values_in, preferred_element_type=jnp.float32
    )
    part_mass = jnp.sum(key_feature.astype(jnp.float32), axis=1)
    state, mass = lax.psum((part_state, part_mass), "sp")
    read = look_up(query_feature, state / count, mass / count)
    mixed = finish_heads(read, count)
    mixed = mixed.reshape(mixed.shape[0], mixed.shape[1], -1)
    return jnp.einsum(
        "btw,wv->btv",
        mixed,
        lax.all_gather(out_weight, "dp", axis=0, tiled=True),
        preferred_element_type=jnp.float32,
    ).astype(jnp.bfloat16)


def solution(mesh):
    placed = (
        P("dp", "sp", None, None),
        P("dp", "sp", None, None),
        P("dp", "sp", None, None),
        P("dp", None),
    )
    return jax.shard_map(
        on_device, mesh=mesh, in_specs=placed, out_specs=P("dp", "sp", None), check_vma=False
    )
```

profile of v0, /device:TPU:0, one launch (start us, length us, event | category | flops | bytes accessed | tf_op | source)
XLA Modules:
  0.0 217.6 jit_solution(422458579611909834)
XLA Ops:
  7.4 0.0 all-reduce.2.cloned.1.call-start
  7.4 9.5 %add_convert_fusion.1 = (bf16[2,1024,16,128]{3,2,1,0:T(8,128)(2,1)}, f32[2,16,128]{2,1,0:T(8,128)S(1)}) fusion(bf16[2,1024,16,128]{3,2,1,0:T(8,128)(2,1)} %param.5), kind=kLoop, calls=%fused_computation.5 | loop fusion | flops 25161728 | bytes 16793600 | tf_op jit(solution)/shard_map/convert_element_type | solution.py:9
  16.8 15.3 %fusion.4 = f32[2,16,128,128]{2,3,1,0:T(8,128)} fusion(bf16[2,1024,16,128]{3,2,1,0:T(8,128)(2,1)} %param.6, bf16[2,1024,16,128]{3,2,1,0:T(8,128)(2,1)} %get-tuple-element.5), kind=kOutput, calls=%fused_computation.8 | convolution fusion | flops 1073741824 | bytes 18874368 | tf_op jit(solution)/shard_map/bthd,bthe->bhde/dot_general | solution.py:30
  32.1 0.0 all-reduce.2.cloned.1.call-update
  32.2 0.2 all-gather.2.cloned.1.call-start
  32.4 0.3 all-gather.2.cloned.1.call-update
  32.7 8.9 %add_convert_fusion = bf16[2,1024,16,128]{3,2,1,0:T(8,128)(2,1)} fusion(bf16[2,1024,16,128]{3,2,1,0:T(8,128)(2,1)} %param.4), kind=kLoop, calls=%fused_computation.4 | loop fusion | flops 16777216 | bytes 16777216 | tf_op jit(solution)/shard_map/convert_element_type | solution.py:9
  41.7 12.7 %copy.10 = bf16[2,1024,16,128]{1,3,2,0:T(8,128)(2,1)} copy(bf16[2,1024,16,128]{3,2,1,0:T(8,128)(2,1)} %add_convert_fusion) | data formatting | bytes 16777216 | tf_op jit(solution)/shard_map/convert_element_type | solution.py:9
  54.3 27.3 %psum.15 = f32[2,16,128]{2,1,0:T(8,128)S(1)} all-reduce(f32[2,16,128]{2,1,0:T(8,128)S(1)} %get-tuple-element.6), channel_id=1, replica_groups=mesh['dp'=4,'sp'=8] {'sp'}, use_global_device_ids=true, to_apply=%region_2.0 | all-reduce | flops 4096 | bytes 32768 | tf_op jit(solution)/shard_map/psum | solution.py:34
  81.7 5.8 %fusion.13 = f32[2,16,1,1024]{3,2,1,0:T(1,128)S(1)} fusion(f32[2,16,128,1]{2,3,1,0:T(1,128)S(1)} %bitcast.25, bf16[2,1024,16,128]{1,3,2,0:T(8,128)(2,1)} %copy.10), kind=kOutput, calls=%fused_computation.18 | convolution fusion | flops 50331648 | bytes 8536064 | tf_op jit(solution)/shard_map/bthd,bhd->bth/dot_general | solution.py:21
  87.5 9.5 %all-reduce.2.cloned.1.call-done = f32[2,16,128,128]{2,3,1,0:T(8,128)} async-done(((f32[2,16,128,128]{2,3,1,0:T(8,128)}), f32[2,16,128,128]{2,3,1,0:T(8,128)}) %all-reduce.2.cloned.1.call-update) | async-done | bytes 2097168 | tf_op jit(solution)/shard_map/psum | solution.py:34
  97.0 9.7 %fusion.1 = bf16[2,1024,16,128]{1,3,2,0:T(8,128)(2,1)} fusion(f32[2,1024,16]{1,2,0:T(8,128)S(1)} %fusion.11, bf16[2,1024,16,128]{1,3,2,0:T(8,128)(2,1)} %copy.10, f32[2,16,128,128]{2,3,1,0:T(8,128)} %all-reduce.2.cloned.1.call-done), kind=kOutput, calls=%fused_computation.2 | convolution fusion | flops 1087373312 | bytes 19005440 | tf_op jit(solution)/shard_map/bthd,bhde->bthe/dot_general | solution.py:18
  106.7 79.8 %all-gather.2.cloned.1.call-done = bf16[2048,2048]{1,0:T(8,128)(2,1)} async-done(((bf16[512,2048]{1,0:T(8,128)(2,1)}), bf16[2048,2048]{1,0:T(8,128)(2,1)}) %all-gather.2.cloned.1.call-update) | async-done | bytes 8388624 | tf_op jit(solution)/shard_map/all_gather | solution.py:41
  186.4 23.7 %fusion.7 = bf16[2,1024,2048]{2,1,0:T(8,128)(2,1)} fusion(bf16[2,1024,2048]{1,2,0:T(8,128)(2,1)} %bitcast.26, bf16[2048,2048]{1,0:T(8,128)(2,1)} %all-gather.2.cloned.1.call-done), kind=kOutput, calls=%fused_computation.11 | convolution fusion | flops 17184063488 | bytes 25165824 | tf_op jit(solution)/shard_map/btw,wv->btv/dot_general | solution.py:38
  (2 shorter events, 0.0 us)
Async XLA Ops:
  7.4 89.6 %all-reduce.2.cloned.1.call-start = ((), (), s32[]{:S(2)}) async-start(), calls=%async_computation | async-start | bytes 4194304 | tf_op jit(solution)/shard_map/psum | solution.py:34
  32.2 154.3 %all-gather.2.cloned.1.call-start = ((), (), s32[]{:S(2)}) async-start(), calls=%async_computation.1 | async-start | bytes 10485760 | tf_op jit(solution)/shard_map/all_gather | solution.py:41
Sparse Core Ops, SparseCore 0:
  32.3 64.6 all-reduce.1
Sparse Core Ops, SparseCore 1:
  34.2 152.2 all-gather.1
where the time goes:
time: 218 us
  waiting for transfers between devices  89.6 us (41%)
  matrix products  54.4 us (25%)
  blocking collectives  27.3 us (13%)
  other arithmetic  18.5 us (8%)
  between operations  14.8 us (7%)
  local copies, waits for them, and re-layouts  12.7 us (6%)
    all_gather x1, waiting for transfers between devices, on_device(): lax.all_gather(out_weight, 'dp', axis=0, tiled=True)  79.8 us
    psum x1, blocking collectives, on_device(): state, mass = lax.psum((part_state, part_mass), 'sp')  27.3 us
    dot_general x1, matrix products, on_device(): jnp.einsum('btw,wv->btv', mixed, lax.all_gather(out_weight, 'dp', axis=0,...  23.7 us
    convert_element_type x2, other arithmetic, feature_map(): return (wide * wide + 0.1).astype(jnp.bfloat16)  18.4 us
    dot_general x1, matrix products, on_device(): jnp.einsum('bthd,bthe->bhde', key_feature, values_in, preferred_element_t...  15.3 us
    convert_element_type x1, local copies, waits for them, and re-layouts, feature_map(): return (wide * wide + 0.1).astype(jnp.bfloat16)  12.7 us
    dot_general x1, matrix products, look_up(): jnp.einsum('bthd,bhde->bthe', features, state.astype(jnp.bfloat16), prefe...  9.66 us
    psum x1, waiting for transfers between devices, on_device(): state, mass = lax.psum((part_state, part_mass), 'sp')  9.49 us
  transfers between devices with their start and end apart: 2, of which 2 were waited for; matrix products, arithmetic and copies ran while one was open for 17% of the time, Pallas kernels for 0%

commit v1 on v0

v1 whole, which is shorter than its diff:
```python
import functools

import jax
import jax.numpy as jnp
from jax import lax
from jax.experimental import pallas as pl
from jax.experimental.pallas import tpu as pltpu
from jax.sharding import PartitionSpec as P

MESH = pl.DeviceIdType.MESH
SLOTS = 3
CHUNK = 256
TILE = 256


def feature_map(values):
    wide = values.astype(jnp.float32)
    return (wide * wide + 0.1).astype(jnp.bfloat16)


def gather_kernel(
    groups, count, chunk, batch, tokens, heads, size,
    k_ref, v_ref, w_ref, state_ref, mass_ref, wide_ref,
    k_buf, v_buf, total, sums, core_in, half_out, half_in, sums_out, sums_in,
    load_sem, own_sem, z_send, z_recv, w_send, w_recv, s_send, s_recv,
):
    depth, lanes = groups
    places = lanes // 2
    levels = places.bit_length() - 1
    d, s = lax.axis_index("dp"), lax.axis_index("sp")
    core, place = s % 2, s // 2
    piece = core * places + place
    rows = w_ref.shape[0]
    part = rows // lanes
    half_width = w_ref.shape[1] // 2
    steps = batch * tokens // chunk
    per_batch = tokens // chunk

    def flip(value, bit):
        return value + (1 << bit) - 2 * (1 << bit) * ((value // (1 << bit)) % 2)

    partners = [flip(s, bit) for bit in range(levels + 1)]

    def to_lane(bit):
        return {"sp": partners[bit]}

    barrier = pltpu.get_barrier_semaphore()
    for bit in range(levels + 1):
        pl.semaphore_signal(barrier, inc=1, device_id=to_lane(bit), device_id_type=MESH)
    for k in range(1, depth):
        pl.semaphore_signal(
            barrier, inc=1, device_id={"dp": (d + k) % depth}, device_id_type=MESH
        )

    def load(i):
        half = steps // 2
        side = jnp.where(i < half, 1 - core, core)
        at = side * half + i % half
        b, t = at // per_batch, at % per_batch
        slot = i % SLOTS
        return (
            pltpu.make_async_copy(
                k_ref.at[b, pl.ds(t * chunk, chunk)], k_buf.at[slot], load_sem.at[0, slot]
            ),
            pltpu.make_async_copy(
                v_ref.at[b, pl.ds(t * chunk, chunk)], v_buf.at[slot], load_sem.at[1, slot]
            ),
        )

    for i in range(min(SLOTS - 1, steps)):
        for copy in load(i):
            copy.start()
    total[...] = jnp.zeros_like(total)
    sums[...] = jnp.zeros_like(sums)
    pl.semaphore_wait(barrier, levels + depth)

    def z_copy(k):
        return pltpu.make_async_remote_copy(
            src_ref=w_ref.at[pl.ds(piece * part, part)],
            dst_ref=wide_ref.at[pl.ds(d * rows + piece * part, part)],
            send_sem=z_send.at[k],
            recv_sem=z_recv.at[k],
            device_id={"dp": (d + k) % depth},
            device_id_type=MESH,
        )

    near = []
    for k in range(1, depth // 2 + 1):
        near += [k] if k == depth - k else [k, depth - k]
    for k in near:
        z_copy(k).start()
    own = pltpu.make_async_copy(w_ref, wide_ref.at[pl.ds(d * rows, rows)], own_sem)
    own.start()

    def orders(side):
        return list(range(levels)) if side == 0 else list(range(levels))[::-1]

    def w_copies(k, stage):
        first = ((d - k) % depth) * rows
        if stage == levels:
            block = wide_ref.at[pl.ds(first + core * places * part, places * part)]
            slot = 2 * (places - 1)
            return [
                pltpu.make_async_remote_copy(
                    src_ref=block, dst_ref=block, send_sem=w_send.at[k, slot],
                    recv_sem=w_recv.at[k, slot], device_id=to_lane(0), device_id_type=MESH,
                )
            ]
        copies = []
        for side in range(2):
            bits = orders(side)
            for subset in range(1 << stage):
                member = place
                for j in range(stage):
                    if subset >> j & 1:
                        member = flip(member, bits[j])
                slot = side * (places - 1) + (1 << stage) - 1 + subset
                block = wide_ref.at[
                    pl.ds(first + (core * places + member) * part, part),
                    pl.ds(side * half_width, half_width),
                ]
                copies.append(
                    pltpu.make_async_remote_copy(
                        src_ref=block, dst_ref=block, send_sem=w_send.at[k, slot],
                        recv_sem=w_recv.at[k, slot], device_id=to_lane(bits[stage] + 1),
                        device_id_type=MESH,
                    )
                )
        return copies

    def w_step(k, stage):
        if stage == 0:
            z_copy(k).wait_recv()
        else:
            for copy in w_copies(k, stage - 1):
                copy.wait_recv()
        for copy in w_copies(k, stage):
            copy.start()

    held = total.shape[0] // 2
    core_copy = pltpu.make_async_remote_copy(
        src_ref=total.at[pl.ds((1 - core) * held, held)], dst_ref=core_in,
        send_sem=s_send.at[0], recv_sem=s_recv.at[0],
        device_id=to_lane(0), device_id_type=MESH,
    )

    def step(i, carry):
        @pl.when(i + SLOTS - 1 < steps)
        def _():
            for copy in load(i + SLOTS - 1):
                copy.start()

        @pl.when(i == steps // 2)
        def _():
            core_copy.start()

        for copy in load(i):
            copy.wait()
        slot = i % SLOTS
        half = steps // 2
        b = (jnp.where(i < half, 1 - core, core) * half + i % half) // per_batch
        k_feature = feature_map(k_buf[slot])
        sums[pl.ds(b * heads, heads), :] += jnp.sum(k_feature.astype(jnp.float32), axis=0)
        k_heads = pltpu.einshape("thd->htd", k_feature)
        v_heads = pltpu.einshape("thd->htd", v_buf[slot])
        for h in range(heads):
            at = pl.ds((b * heads + h) * size, size)
            total[at, :] += lax.dot_general(
                k_heads[h], v_heads[h], (((0,), (0,)), ((), ())),
                preferred_element_type=jnp.float32,
            )
        return carry

    lax.fori_loop(0, steps, step, 0)

    def mass_copy(stage):
        bit = 0 if stage == 0 else orders(0)[stage - 1] + 1
        return pltpu.make_async_remote_copy(
            src_ref=sums_out.at[stage], dst_ref=sums_in.at[stage],
            send_sem=s_send.at[1 + stage], recv_sem=s_recv.at[1 + stage],
            device_id=to_lane(bit), device_id_type=MESH,
        )

    def mass_send(stage):
        sums_out[stage] = sums[...]
        mass_copy(stage).start()

    def mass_take(stage):
        mass_copy(stage).wait()
        sums[...] += sums_in[stage]

    mass_send(0)
    core_copy.wait()
    mine = pl.ds(core * held, held)
    total[mine, :] += core_in[...]
    mass_take(0)

    quarter = held // 2
    starts = [[core * held + side * quarter] for side in range(2)]

    def reduce_copy(stage, side):
        length = quarter >> (stage + 1)
        slot = 2 + levels + 2 * stage + side
        base = side * quarter + quarter - 2 * length
        return pltpu.make_async_remote_copy(
            src_ref=half_out.at[pl.ds(base, length)], dst_ref=half_in.at[pl.ds(base, length)],
            send_sem=s_send.at[slot], recv_sem=s_recv.at[slot],
            device_id=to_lane(orders(side)[stage] + 1), device_id_type=MESH,
        )

    def reduce_send(stage):
        length = quarter >> (stage + 1)
        for side in range(2):
            first = starts[side][stage]
            upper = (place // (1 << orders(side)[stage])) % 2
            keep, give = first + upper * length, first + (1 - upper) * length
            starts[side].append(keep)
            base = side * quarter + quarter - 2 * length
            half_out[pl.ds(base, length), :] = total[pl.ds(give, length), :].astype(jnp.bfloat16)
            reduce_copy(stage, side).start()
        mass_send(stage + 1)

    def reduce_take(stage):
        length = quarter >> (stage + 1)
        for side in range(2):
            base = side * quarter + quarter - 2 * length
            reduce_copy(stage, side).wait()
            total[pl.ds(starts[side][stage + 1], length), :] += half_in[
                pl.ds(base, length), :
            ].astype(jnp.float32)
        mass_take(stage + 1)

    def spread_copy(stage, side):
        length = quarter >> (stage + 1)
        block = state_ref.at[pl.ds(starts[side][stage + 1], length)]
        slot = 2 + 3 * levels + 2 * stage + side
        return pltpu.make_async_remote_copy(
            src_ref=block, dst_ref=block, send_sem=s_send.at[slot], recv_sem=s_recv.at[slot],
            device_id=to_lane(orders(side)[stage] + 1), device_id_type=MESH,
        )

    final_copy = pltpu.make_async_remote_copy(
        src_ref=state_ref.at[mine], dst_ref=state_ref.at[mine],
        send_sem=s_send.at[2 + 5 * levels], recv_sem=s_recv.at[2 + 5 * levels],
        device_id=to_lane(0), device_id_type=MESH,
    )

    todo = [(k, stage) for k in near[:2] for stage in range(1)]
    later = [(k, 0) for k in near[2:]]
    for stage in range(1, levels + 1):
        later += [(k, stage) for k in near]
    todo += later

    def next_w(amount=1):
        for _ in range(amount):
            if todo:
                w_step(*todo.pop(0))

    for stage in range(levels):
        reduce_send(stage)
        next_w()
        reduce_take(stage)
    length = quarter >> levels
    for side in range(2):
        at = pl.ds(starts[side][levels], length)
        state_ref[at, :] = (total[at, :] / count).astype(jnp.bfloat16)
    mass_ref[...] = sums[...] / count
    for stage in reversed(range(levels)):
        for side in range(2):
            spread_copy(stage, side).start()
        next_w()
        for side in range(2):
            spread_copy(stage, side).wait()
    final_copy.start()
    next_w(len(todo))
    final_copy.wait()
    for k in near:
        z_copy(k).wait_send()
        for stage in range(levels + 1):
            for copy in w_copies(k, stage):
                copy.wait_send()
                if stage == levels:
                    copy.wait_recv()
    own.wait()


def gather(queries, keys_in, values_in, out_weight, count):
    batch, tokens, heads, size = keys_in.shape
    depth, lanes = lax.axis_size("dp"), lax.axis_size("sp")
    places = lanes // 2
    levels = places.bit_length() - 1
    rows, width = out_weight.shape
    area = batch * heads * size
    chunk = min(CHUNK, tokens)
    any_space = pl.BlockSpec(memory_space=pl.ANY)
    vmem = pl.BlockSpec(memory_space=pltpu.VMEM)
    dma = pltpu.SemaphoreType.DMA
    f32, bf16 = jnp.float32, jnp.bfloat16
    return pl.pallas_call(
        functools.partial(
            gather_kernel, (depth, lanes), count, chunk, batch, tokens, heads, size
        ),
        out_shape=(
            jax.ShapeDtypeStruct((area, size), bf16),
            jax.ShapeDtypeStruct((batch * heads, size), f32),
            jax.ShapeDtypeStruct((depth * rows, width), bf16),
        ),
        in_specs=[any_space, any_space, vmem],
        out_specs=(vmem, vmem, any_space),
        scratch_shapes=[
            pltpu.VMEM((SLOTS, chunk, heads, size), bf16),
            pltpu.VMEM((SLOTS, chunk, heads, size), bf16),
            pltpu.VMEM((area, size), f32),
            pltpu.VMEM((batch * heads, size), f32),
            pltpu.VMEM((area // 2, size), f32),
            pltpu.VMEM((area // 2, size), bf16),
            pltpu.VMEM((area // 2, size), bf16),
            pltpu.VMEM((levels + 1, batch * heads, size), f32),
            pltpu.VMEM((levels + 1, batch * heads, size), f32),
            dma((2, SLOTS)),
            dma,
            dma((depth,)),
            dma((depth,)),
            dma((depth, 2 * places - 1)),
            dma((depth, 2 * places - 1)),
            dma((3 + 5 * levels,)),
            dma((3 + 5 * levels,)),
        ],
        compiler_params=pltpu.CompilerParams(
            collective_id=0, has_side_effects=True, vmem_limit_bytes=60 * 2**20
        ),
    )(keys_in, values_in, out_weight)


def project_kernel(count, q_ref, state_ref, mass_ref, w_ref, out_ref, table, mixed):
    heads, size = q_ref.shape[2:]
    tile = q_ref.shape[1]
    f32, bf16 = jnp.float32, jnp.bfloat16

    @pl.when(pl.program_id(1) == 0)
    def _():
        b = pl.program_id(0)
        for h in range(heads):
            line = mass_ref[pl.ds(b * heads + h, 1), :]
            column = jnp.transpose(jnp.broadcast_to(line, (size, size)))
            high = column.astype(bf16)
            table[h, :size, :size] = state_ref[pl.ds((b * heads + h) * size, size), :]
            table[h, :size, size:] = high
            table[h, size:, :size] = jnp.zeros((size, size), bf16)
            table[h, size:, size:] = (column - high.astype(f32)).astype(bf16)

    q_heads = pltpu.einshape("thd->htd", feature_map(q_ref[0]))
    for h in range(heads):
        feature = q_heads[h]
        both = jnp.dot(
            jnp.concatenate([feature, feature], axis=1), table[h], preferred_element_type=f32
        )
        read = both[:, :size] / (both[:, size:] + 0.001)
        mixed[:, h * size : (h + 1) * size] = (read * count**0.5).astype(bf16)
    out_ref[0] = jnp.dot(mixed[...], w_ref[...], preferred_element_type=f32).astype(bf16)


def project(queries_in, state, mass, wide, count):
    batch, tokens, heads, size = queries_in.shape
    width = wide.shape[1]
    tile = min(TILE, tokens)
    return pl.pallas_call(
        functools.partial(project_kernel, count),
        grid=(batch, tokens // tile),
        out_shape=jax.ShapeDtypeStruct((batch, tokens, width), jnp.bfloat16),
        in_specs=[
            pl.BlockSpec((1, tile, heads, size), lambda b, t: (b, t, 0, 0)),
            pl.BlockSpec(memory_space=pltpu.VMEM),
            pl.BlockSpec(memory_space=pltpu.VMEM),
            pl.BlockSpec(memory_space=pltpu.VMEM),
        ],
        out_specs=pl.BlockSpec((1, tile, width), lambda b, t: (b, t, 0)),
        scratch_shapes=[
            pltpu.VMEM((heads, 2 * size, 2 * size), jnp.bfloat16),
            pltpu.VMEM((tile, heads * size), jnp.bfloat16),
        ],
        compiler_params=pltpu.CompilerParams(
            dimension_semantics=("arbitrary", "arbitrary"), vmem_limit_bytes=60 * 2**20
        ),
    )(queries_in, state, mass, wide)


def on_device(queries_in, keys_in, values_in, out_weight):
    count = queries_in.shape[1] * lax.axis_size("sp")
    state, mass, wide = gather(queries_in, keys_in, values_in, out_weight, count)
    return project(queries_in, state, mass, wide, count)


def solution(mesh):
    placed = (
        P("dp", "sp", None, None),
        P("dp", "sp", None, None),
        P("dp", "sp", None, None),
        P("dp", None),
    )
    return jax.shard_map(
        on_device, mesh=mesh, in_specs=placed, out_specs=P("dp", "sp", None), check_vma=False
    )
```

time: 218 us -> 91.4 us (0.42)
  Pallas kernels: 0 us -> 91.2 us
  waiting for transfers between devices: 89.6 us -> 0 us
  matrix products: 54.4 us -> 0 us
  blocking collectives: 27.3 us -> 0 us
  other arithmetic: 18.5 us -> 0 us
  between operations: 14.8 us -> 0.01 us
  local copies, waits for them, and re-layouts: 12.7 us -> 0 us
    pallas_call x0 -> x2, Pallas kernels: none -> 91.2 us  [the longest x1 59.9 us: gather(): pl.pallas_call(functools.partial(gather_kernel, (depth, lanes), count, ch...]
    all_gather x1 -> x0, waiting for transfers between devices: 79.8 us -> none  [on_device(): lax.all_gather(out_weight, 'dp', axis=0, tiled=True)]
    dot_general x4 -> x0, matrix products: 54.4 us -> none  [the longest x1 23.7 us: on_device(): jnp.einsum('btw,wv->btv', mixed, lax.all_gather(out_weight, 'dp', axis=0,...]
    psum x1 -> x0, blocking collectives: 27.3 us -> none  [on_device(): state, mass = lax.psum((part_state, part_mass), 'sp')]
    convert_element_type x2 -> x0, other arithmetic: 18.4 us -> none  [feature_map(): return (wide * wide + 0.1).astype(jnp.bfloat16)]
    convert_element_type x1 -> x0, local copies, waits for them, and re-layouts: 12.7 us -> none  [feature_map(): return (wide * wide + 0.1).astype(jnp.bfloat16)]
    psum x1 -> x0, waiting for transfers between devices: 9.49 us -> none  [on_device(): state, mass = lax.psum((part_state, part_mass), 'sp')]
  transfers between devices with their start and end apart: 2 -> 0, of which waited for: 2 -> 0; matrix products, arithmetic and copies ran while one was open for 17% -> 0% of each run, Pallas kernels for 0% -> 0%
where the time goes in v1:
time: 91.4 us; the launch traced here: 91.2 us
  Pallas kernels  91.2 us (100%)
    pallas_call x1, Pallas kernels, gather(): pl.pallas_call(functools.partial(gather_kernel, (depth, lanes), count, ch...  59.9 us
    pallas_call x1, Pallas kernels, project(): pl.pallas_call(functools.partial(project_kernel, count), grid=(batch, tok...  31.3 us

profile of v1, /device:TPU:0, one launch (start us, length us, event | category | flops | bytes accessed | tf_op | source)
XLA Modules:
  0.0 91.2 jit_solution(6541823833661831529)
XLA Ops:
  0.0 59.9 %shard_map.46 = (bf16[4096,128]{1,0:T(8,128)(2,1)}, f32[32,128]{1,0:T(8,128)}, bf16[2048,2048]{1,0:T(8,128)(2,1)}) custom-call(bf16[2,1024,16,128]{3,2,1,0:T(8,128)(2,1)} %k_ref.1, bf16[2,1024,16,128]{3,2,1,0:T(8,128)(2,1)} %v_ref.1, bf16[512,2048]{1,0:T(8,128)(2,1)} %w_ref.1), custom_call_target="tpu_custom_call" | custom-call | tf_op jit(solution)/shard_map/pallas_call | solution.py:299
  60.0 31.3 %shard_map.47 = bf16[2,1024,2048]{2,1,0:T(8,128)(2,1)} custom-call(bf16[2,1024,16,128]{3,2,1,0:T(8,128)(2,1)} %q_ref.1, bf16[4096,128]{1,0:T(8,128)(2,1)} %get-tuple-element.8.state_ref, f32[32,128]{1,0:T(8,128)} %get-tuple-element.9.mass_ref, bf16[2048,2048]{1,0:T(8,128)(2,1)} %get-tuple-element.10.w_ref), custom_call_target="tpu_custom_call" | custom-call | tf_op jit(solution)/shard_map/pallas_call | solution.py:367

commit v2 on v1

--- a/solution.py
+++ b/solution.py
@@ -47,7 +47,7 @@
     barrier = pltpu.get_barrier_semaphore()
     for bit in range(levels + 1):
         pl.semaphore_signal(barrier, inc=1, device_id=to_lane(bit), device_id_type=MESH)
-    for k in range(1, depth):
+    for k in (1, depth - 1):
         pl.semaphore_signal(
             barrier, inc=1, device_id={"dp": (d + k) % depth}, device_id_type=MESH
         )
@@ -72,31 +72,42 @@
             copy.start()
     total[...] = jnp.zeros_like(total)
     sums[...] = jnp.zeros_like(sums)
-    pl.semaphore_wait(barrier, levels + depth)
-
-    def z_copy(k):
+    pl.semaphore_wait(barrier, levels + 3)
+
+    def origin(way, hop):
+        return d - hop if way == 0 else d + hop
+
+    def inside(place_on_dp):
+        return jnp.logical_and(place_on_dp >= 0, place_on_dp < depth)
+
+    def z_copy(way, hop):
+        at = pl.ds(origin(way, hop - 1) * rows + piece * part, part)
         return pltpu.make_async_remote_copy(
-            src_ref=w_ref.at[pl.ds(piece * part, part)],
-            dst_ref=wide_ref.at[pl.ds(d * rows + piece * part, part)],
-            send_sem=z_send.at[k],
-            recv_sem=z_recv.at[k],
-            device_id={"dp": (d + k) % depth},
+            src_ref=w_ref.at[pl.ds(piece * part, part)] if hop == 1 else wide_ref.at[at],
+            dst_ref=wide_ref.at[at],
+            send_sem=z_send.at[way, hop],
+            recv_sem=z_recv.at[way, hop],
+            device_id={"dp": (d + (1 if way == 0 else depth - 1)) % depth},
             device_id_type=MESH,
         )
 
-    near = []
-    for k in range(1, depth // 2 + 1):
-        near += [k] if k == depth - k else [k, depth - k]
-    for k in near:
-        z_copy(k).start()
+    def sends(way, hop):
+        return jnp.logical_and(inside(origin(way, hop - 1)), inside(origin(way, -1)))
+
+    def z_start(hop):
+        for way in range(2):
+            pl.when(sends(way, hop))(lambda way=way: z_copy(way, hop).start())
+
+    z_start(1)
     own = pltpu.make_async_copy(w_ref, wide_ref.at[pl.ds(d * rows, rows)], own_sem)
     own.start()
 
     def orders(side):
         return list(range(levels)) if side == 0 else list(range(levels))[::-1]
 
-    def w_copies(k, stage):
-        first = ((d - k) % depth) * rows
+    def w_copies(way, hop, stage):
+        first = origin(way, hop) * rows
+        k = way * depth + hop
         if stage == levels:
             block = wide_ref.at[pl.ds(first + core * places * part, places * part)]
             slot = 2 * (places - 1)
@@ -128,14 +139,34 @@
                 )
         return copies
 
-    def w_step(k, stage):
-        if stage == 0:
-            z_copy(k).wait_recv()
-        else:
-            for copy in w_copies(k, stage - 1):
-                copy.wait_recv()
-        for copy in w_copies(k, stage):
-            copy.start()
+    def w_step(hop, stage):
+        def arrived(way):
+            if stage == 0:
+                at = pl.ds(origin(way, hop) * rows + piece * part, part)
+                pltpu.make_async_remote_copy(
+                    src_ref=wide_ref.at[at], dst_ref=wide_ref.at[at],
+                    send_sem=z_send.at[way, hop], recv_sem=z_recv.at[way, hop],
+                    device_id={"dp": (d + 1) % depth}, device_id_type=MESH,
+                ).wait_recv()
+            else:
+                for copy in w_copies(way, hop, stage - 1):
+                    copy.wait_recv()
+
+        def forward(way):
+            for copy in w_copies(way, hop, stage):
+                copy.start()
+
+        for act in (arrived, None, forward):
+            if act is None:
+                if stage == 0 and hop + 1 < depth:
+                    z_start(hop + 1)
+                continue
+            for way in range(2):
+                pl.when(inside(origin(way, hop)))(functools.partial(act, way))
+
+    todo = [(hop, stage) for hop in range(1, depth) for stage in range(levels + 1)]
+    todo.sort(key=lambda item: (item[0] + item[1], item[0]))
+    early = {steps // 2: todo.pop(0), steps - 2: todo.pop(0), steps - 1: todo.pop(0)}
 
     held = total.shape[0] // 2
     core_copy = pltpu.make_async_remote_copy(
@@ -153,6 +184,9 @@
         @pl.when(i == steps // 2)
         def _():
             core_copy.start()
+
+        for moment, item in early.items():
+            pl.when(i == moment)(functools.partial(w_step, *item))
 
         for copy in load(i):
             copy.wait()
@@ -245,12 +279,6 @@
         device_id=to_lane(0), device_id_type=MESH,
     )
 
-    todo = [(k, stage) for k in near[:2] for stage in range(1)]
-    later = [(k, 0) for k in near[2:]]
-    for stage in range(1, levels + 1):
-        later += [(k, stage) for k in near]
-    todo += later
-
     def next_w(amount=1):
         for _ in range(amount):
             if todo:
@@ -258,7 +286,7 @@
 
     for stage in range(levels):
         reduce_send(stage)
-        next_w()
+        next_w(2 - stage)
         reduce_take(stage)
     length = quarter >> levels
     for side in range(2):
@@ -274,13 +302,18 @@
     final_copy.start()
     next_w(len(todo))
     final_copy.wait()
-    for k in near:
-        z_copy(k).wait_send()
-        for stage in range(levels + 1):
-            for copy in w_copies(k, stage):
-                copy.wait_send()
-                if stage == levels:
-                    copy.wait_recv()
+    for hop in range(1, depth):
+        for way in range(2):
+            pl.when(sends(way, hop))(lambda way=way, hop=hop: z_copy(way, hop).wait_send())
+
+            @pl.when(inside(origin(way, hop)))
+            def _(way=way, hop=hop):
+                for stage in range(levels + 1):
+                    for copy in w_copies(way, hop, stage):
+                        copy.wait_send()
+                        if stage == levels:
+                            copy.wait_recv()
+
     own.wait()
 
 
@@ -319,10 +352,10 @@
             pltpu.VMEM((levels + 1, batch * heads, size), f32),
             dma((2, SLOTS)),
             dma,
-            dma((depth,)),
-            dma((depth,)),
-            dma((depth, 2 * places - 1)),
-            dma((depth, 2 * places - 1)),
+            dma((2, depth)),
+            dma((2, depth)),
+            dma((2 * depth, 2 * places - 1)),
+            dma((2 * depth, 2 * places - 1)),
             dma((3 + 5 * levels,)),
             dma((3 + 5 * levels,)),
         ],
@@ -332,14 +365,19 @@
     )(keys_in, values_in, out_weight)
 
 
-def project_kernel(count, q_ref, state_ref, mass_ref, w_ref, out_ref, table, mixed):
-    heads, size = q_ref.shape[2:]
-    tile = q_ref.shape[1]
+def project_kernel(
+    count, per_batch, q_ref, state_ref, mass_ref, w_hbm, out_ref, table, mixed, w_ref, w_sem
+):
+    heads, size = q_ref.shape[1:]
     f32, bf16 = jnp.float32, jnp.bfloat16
-
-    @pl.when(pl.program_id(1) == 0)
+    i, last = pl.program_id(0), pl.num_programs(0) - 1
+    load = pltpu.make_async_copy(w_hbm, w_ref, w_sem)
+
+    pl.when(i == 0)(load.start)
+
+    @pl.when(jnp.logical_and(i % per_batch == 0, i < last))
     def _():
-        b = pl.program_id(0)
+        b = i // per_batch
         for h in range(heads):
             line = mass_ref[pl.ds(b * heads + h, 1), :]
             column = jnp.transpose(jnp.broadcast_to(line, (size, size)))
@@ -349,40 +387,63 @@
             table[h, size:, :size] = jnp.zeros((size, size), bf16)
             table[h, size:, size:] = (column - high.astype(f32)).astype(bf16)
 
-    q_heads = pltpu.einshape("thd->htd", feature_map(q_ref[0]))
-    for h in range(heads):
-        feature = q_heads[h]
-        both = jnp.dot(
-            jnp.concatenate([feature, feature], axis=1), table[h], preferred_element_type=f32
-        )
-        read = both[:, :size] / (both[:, size:] + 0.001)
-        mixed[:, h * size : (h + 1) * size] = (read * count**0.5).astype(bf16)
-    out_ref[0] = jnp.dot(mixed[...], w_ref[...], preferred_element_type=f32).astype(bf16)
+    def read(slot):
+        q_heads = pltpu.einshape("thd->htd", feature_map(q_ref[...]))
+        for h in range(heads):
+            feature = q_heads[h]
+            both = jnp.dot(
+                jnp.concatenate([feature, feature], axis=1), table[h], preferred_element_type=f32
+            )
+            top = both[:, :size] / (both[:, size:] + 0.001)
+            mixed[slot, :, h * size : (h + 1) * size] = (top * count**0.5).astype(bf16)
+
+    def finish(slot):
+        out_ref[...] = jnp.dot(mixed[slot], w_ref[...], preferred_element_type=f32).astype(bf16)
+
+    @pl.when(i == 0)
+    def _():
+        read(0)
+        load.wait()
+
+    for slot in range(2):
+        @pl.when(jnp.logical_and(i % 2 == slot, jnp.logical_and(i > 0, i < last)))
+        def _():
+            finish(1 - slot)
+            read(slot)
+
+        @pl.when(jnp.logical_and(i % 2 == slot, i == last))
+        def _():
+            finish(1 - slot)
 
 
 def project(queries_in, state, mass, wide, count):
     batch, tokens, heads, size = queries_in.shape
     width = wide.shape[1]
     tile = min(TILE, tokens)
-    return pl.pallas_call(
-        functools.partial(project_kernel, count),
-        grid=(batch, tokens // tile),
-        out_shape=jax.ShapeDtypeStruct((batch, tokens, width), jnp.bfloat16),
+    tiles = batch * tokens // tile
+    vmem = pl.BlockSpec(memory_space=pltpu.VMEM)
+    out = pl.pallas_call(
+        functools.partial(project_kernel, count, tokens // tile),
+        grid=(tiles + 1,),
+        out_shape=jax.ShapeDtypeStruct((batch * tokens, width), jnp.bfloat16),
         in_specs=[
-            pl.BlockSpec((1, tile, heads, size), lambda b, t: (b, t, 0, 0)),
-            pl.BlockSpec(memory_space=pltpu.VMEM),
-            pl.BlockSpec(memory_space=pltpu.VMEM),
-            pl.BlockSpec(memory_space=pltpu.VMEM),
+            pl.BlockSpec((tile, heads, size), lambda i: (jnp.minimum(i, tiles - 1), 0, 0)),
+            vmem,
+            vmem,
+            pl.BlockSpec(memory_space=pl.ANY),
         ],
-        out_specs=pl.BlockSpec((1, tile, width), lambda b, t: (b, t, 0)),
+        out_specs=pl.BlockSpec((tile, width), lambda i: (jnp.maximum(i - 1, 0), 0)),
         scratch_shapes=[
             pltpu.VMEM((heads, 2 * size, 2 * size), jnp.bfloat16),
-            pltpu.VMEM((tile, heads * size), jnp.bfloat16),
+            pltpu.VMEM((2, tile, heads * size), jnp.bfloat16),
+            pltpu.VMEM(wide.shape, jnp.bfloat16),
+            pltpu.SemaphoreType.DMA,
         ],
         compiler_params=pltpu.CompilerParams(
-            dimension_semantics=("arbitrary", "arbitrary"), vmem_limit_bytes=60 * 2**20
+            dimension_semantics=("arbitrary",), vmem_limit_bytes=60 * 2**20
         ),
-    )(queries_in, state, mass, wide)
+    )(queries_in.reshape(batch * tokens, heads, size), state, mass, wide)
+    return out.reshape(batch, tokens, width)
 
 
 def on_device(queries_in, keys_in, values_in, out_weight):

time: 91.4 us -> 88.6 us (0.969)
  the two profiles are of different devices: /device:TPU:0 before, /device:TPU:9 now
where the time goes in v2:
time: 88.6 us; the launch traced here: 88.4 us
  Pallas kernels  88.4 us (100%)
    pallas_call x1, Pallas kernels, gather(): pl.pallas_call(functools.partial(gather_kernel, (depth, lanes), count, ch...  57.5 us
    pallas_call x1, Pallas kernels, project(): pl.pallas_call(functools.partial(project_kernel, count, tokens // tile),...  30.9 us

profile of v2, /device:TPU:9, one launch (start us, length us, event | category | flops | bytes accessed | tf_op | source)
XLA Modules:
  0.0 88.4 jit_solution(6458639073547257528)
XLA Ops:
  0.0 57.5 %shard_map.46 = (bf16[4096,128]{1,0:T(8,128)(2,1)}, f32[32,128]{1,0:T(8,128)}, bf16[2048,2048]{1,0:T(8,128)(2,1)}) custom-call(bf16[2,1024,16,128]{3,2,1,0:T(8,128)(2,1)} %k_ref.1, bf16[2,1024,16,128]{3,2,1,0:T(8,128)(2,1)} %v_ref.1, bf16[512,2048]{1,0:T(8,128)(2,1)} %w_ref.1), custom_call_target="tpu_custom_call" | custom-call | tf_op jit(solution)/shard_map/pallas_call | solution.py:332
  57.5 30.9 %shard_map.47 = bf16[2048,2048]{1,0:T(8,128)(2,1)} custom-call(bf16[2048,16,128]{2,1,0:T(8,128)(2,1)} %bitcast.2, bf16[4096,128]{1,0:T(8,128)(2,1)} %get-tuple-element.8.state_ref, f32[32,128]{1,0:T(8,128)} %get-tuple-element.9.mass_ref, bf16[2048,2048]{1,0:T(8,128)(2,1)} %get-tuple-element.10.w_hbm), custom_call_target="tpu_custom_call" | custom-call | tf_op jit(solution)/shard_map/pallas_call | solution.py:425

commit v3 on v2

--- a/solution.py
+++ b/solution.py
@@ -10,7 +10,7 @@
 MESH = pl.DeviceIdType.MESH
 SLOTS = 3
 CHUNK = 256
-TILE = 256
+TILE = 512
 
 
 def feature_map(values):

time: 88.6 us -> 88.1 us (level)
  no operation moved by 1% of the time
where the time goes in v3:
time: 88.1 us; the launch traced here: 87.9 us
  Pallas kernels  87.8 us (100%)
    pallas_call x1, Pallas kernels, gather(): pl.pallas_call(functools.partial(gather_kernel, (depth, lanes), count, ch...  57.5 us
    pallas_call x1, Pallas kernels, project(): pl.pallas_call(functools.partial(project_kernel, count, tokens // tile),...  30.2 us

profile of v3, /device:TPU:9, one launch (start us, length us, event | category | flops | bytes accessed | tf_op | source)
XLA Modules:
  0.0 87.9 jit_solution(5737382494464967032)
XLA Ops:
  0.0 57.5 %shard_map.46 = (bf16[4096,128]{1,0:T(8,128)(2,1)}, f32[32,128]{1,0:T(8,128)}, bf16[2048,2048]{1,0:T(8,128)(2,1)}) custom-call(bf16[2,1024,16,128]{3,2,1,0:T(8,128)(2,1)} %k_ref.1, bf16[2,1024,16,128]{3,2,1,0:T(8,128)(2,1)} %v_ref.1, bf16[512,2048]{1,0:T(8,128)(2,1)} %w_ref.1), custom_call_target="tpu_custom_call" | custom-call | tf_op jit(solution)/shard_map/pallas_call | solution.py:332
  57.5 30.2 %shard_map.47 = bf16[2048,2048]{1,0:T(8,128)(2,1)} custom-call(bf16[2048,16,128]{2,1,0:T(8,128)(2,1)} %bitcast.2, bf16[4096,128]{1,0:T(8,128)(2,1)} %get-tuple-element.8.state_ref, f32[32,128]{1,0:T(8,128)} %get-tuple-element.9.mass_ref, bf16[2048,2048]{1,0:T(8,128)(2,1)} %get-tuple-element.10.w_hbm), custom_call_target="tpu_custom_call" | custom-call | tf_op jit(solution)/shard_map/pallas_call | solution.py:425
